TPU v7x, 32 devices: a whole 2x2x4 slice. The times are simulated.
32 devices in a mesh: rep: 4 (over z), own: 8 (over y, x, core).
Axes of the slice: x: 2, y: 2, z: 4, core: 2. Of those that a mesh axis runs over, the one named last changes fastest.
Arguments:
- inputs: bfloat16 [8192, 8192], P(('rep', 'own')), may hold values from -6 to 6
- cotangent: bfloat16 [8192, 8192], P(('rep', 'own')), may hold values from -6 to 6
- gate: float32 [8192], P(('rep', 'own')), may hold values from 0.05 to 0.95
- down_weight: bfloat16 [8192, 256], P('rep'), may hold values from -0.0625 to 0.0625
- up_weight: bfloat16 [8192, 256], P('rep'), may hold values from -0.0625 to 0.0625
- mixing: bfloat16 [256, 256], replicated, may hold values from -0.375 to 0.375
- owner_table: int32 [8, 8], replicated, may hold values from -1 to 31, as said below
- left_factor: float32 [64, 256, 256], P('own'), as said below
- right_factor: float32 [64, 256, 256], P('own'), as said below
Outputs:
- preconditioned: float32 [16384, 256], P('own')
Inputs may be any that keep to these rules, and one draw needn't show every extreme that they name: `owner_table`: each of the 32 block ids stands in exactly one slot; -1 marks an empty slot; some owner has all 8 slots filled. `left_factor`: every slot's matrix is symmetric positive definite. `right_factor`: every slot's matrix is symmetric positive definite.
All inputs are finite; a program needn't handle non-finite values.
Results may differ from a plain program's by a relative error of at most 0.0077.
Values may be sent and summed in bfloat16 or wider, within the bound.
No kernel may reach another device: no remote copies, remote signals or barrier semaphores. Data moves between devices by JAX's collectives and lax.ppermute only.
A program may use at most 128 MiB of HBM per device.

v0:
```python
import jax
import jax.numpy as jnp
from jax import lax
from jax.sharding import PartitionSpec as P

R = 256
ITERS = 5
BETA = 0.95
EPS = 1e-06


def batched(left, right):
    return jnp.einsum("kij,kjl->kil", left, right, precision=lax.Precision.HIGHEST)


def inverse_root(matrices):
    width = matrices.shape[-1]
    identity = jnp.eye(width, dtype=jnp.float32)
    shifted = matrices + EPS * identity
    norm_size = jnp.sqrt(jnp.sum(shifted * shifted, axis=(1, 2)))
    result = jnp.broadcast_to(identity, shifted.shape) * (norm_size ** (-0.25))[:, None, None]
    normed = shifted / norm_size[:, None, None]
    for sweep in range(ITERS):
        factor = (5.0 * identity - normed) / 4.0
        result = batched(result, factor)
        square = batched(factor, factor)
        normed = batched(batched(square, square), normed)
    return result


def shards(
    inputs, cotangent, gate, down_weight, up_weight, mixing, owner_table, left_factor, right_factor
):
    token_total = inputs.shape[0] * lax.axis_size("rep") * lax.axis_size("own")
    slot_count = left_factor.shape[0]
    lifted = (gate[:, None] * inputs.astype(jnp.float32) * cotangent.astype(jnp.float32)).astype(
        jnp.bfloat16
    )
    columns = inputs
    projected = jnp.dot(
        columns,
        lax.all_gather(down_weight, "rep", axis=0, tiled=True),
        preferred_element_type=jnp.float32,
    )
    back_proj = jnp.dot(
        lifted,
        lax.all_gather(up_weight, "rep", axis=0, tiled=True),
        preferred_element_type=jnp.float32,
    )
    inner_act = jnp.tanh(projected).astype(jnp.bfloat16)
    outer_act = jnp.tanh(jnp.dot(inner_act, mixing, preferred_element_type=jnp.float32))
    outer_slope = (back_proj * (1.0 - outer_act * outer_act)).astype(jnp.bfloat16)
    through = lax.dot_general(
        outer_slope, mixing, (((1,), (1,)), ((), ())), preferred_element_type=jnp.float32
    )
    inner_wide = inner_act.astype(jnp.float32)
    signal = (through * (1.0 - inner_wide * inner_wide)).astype(jnp.bfloat16)
    columns = inputs
    shard = lax.psum_scatter(
        lax.dot_general(
            columns, signal, (((0,), (0,)), ((), ())), preferred_element_type=jnp.float32
        )
        / token_total,
        "own",
        scatter_dimension=0,
        tiled=True,
    )
    shard = lax.psum(shard, "rep")
    my_blocks = lax.dynamic_index_in_dim(owner_table, lax.axis_index("own"), 0, keepdims=False)
    wanted = (
        jnp.maximum(my_blocks, 0)[:, None] * R + jnp.arange(R, dtype=jnp.int32)[None, :]
    ).reshape(-1)
    shard_rows = lax.all_gather(shard, "own", axis=0, tiled=True)
    row_total = shard_rows.shape[0]
    inside = (wanted >= 0) & (wanted < row_total)
    selected = jnp.take(shard_rows, jnp.clip(wanted, 0, row_total - 1), axis=0)
    owned = jnp.where(inside[:, None], selected, jnp.zeros((slot_count * R, R), jnp.float32))
    my_row = lax.dynamic_index_in_dim(owner_table, lax.axis_index("own"), 0, keepdims=False)
    filled_slots = (my_row >= 0)[:, None, None]
    gradients = jnp.where(filled_slots, owned.reshape(slot_count, R, R), 0.0)
    flipped = jnp.swapaxes(gradients, 1, 2)
    left_new = BETA * left_factor + (1.0 - BETA) * batched(gradients, flipped)
    right_new = BETA * right_factor + (1.0 - BETA) * batched(flipped, gradients)
    factors = jnp.concatenate([left_new, right_new], axis=0)
    inverse_roots = inverse_root(factors)
    preconditioned = batched(
        batched(inverse_roots[:slot_count], gradients), inverse_roots[slot_count:]
    )
    return jnp.where(filled_slots, preconditioned, 0.0).reshape(slot_count * R, R)


def solution(mesh):
    in_specs = (
        P(("rep", "own"), None),
        P(("rep", "own"), None),
        P(("rep", "own")),
        P("rep", None),
        P("rep", None),
        P(),
        P(),
        P("own", None, None),
        P("own", None, None),
    )
    out_specs = P("own", None)
    return jax.shard_map(shards, mesh=mesh, in_specs=in_specs, out_specs=out_specs, check_vma=False)
```

profile of v0, /device:TPU:0, one launch (start us, length us, event | category | flops | bytes accessed | tf_op | source)
XLA Modules:
  0.0 500.8 jit_solution(6470604852635249459)
XLA Ops:
  6.5 0.7 all-gather.6.cloned.1.call-update
  7.3 0.0 all-gather.4.cloned.1.call-start
  7.3 0.7 all-gather.4.cloned.1.call-update
  8.0 0.0 reduce-scatter.2.cloned.1.call-start
  8.1 84.3 %all-gather.6.cloned.1.call-done = bf16[8192,256]{1,0:T(8,128)(2,1)} async-done(((bf16[2048,256]{1,0:T(8,128)(2,1)}), bf16[8192,256]{1,0:T(8,128)(2,1)}) %all-gather.6.cloned.1.call-update) | async-done | bytes 4194320 | tf_op jit(solution)/shard_map/all_gather | solution.py:42
  92.4 4.7 fusion.47
  97.1 76.1 %all-gather.4.cloned.1.call-done = bf16[8192,256]{1,0:T(8,128)(2,1)} async-done(((bf16[2048,256]{1,0:T(8,128)(2,1)}), bf16[8192,256]{1,0:T(8,128)(2,1)}) %all-gather.4.cloned.1.call-update) | async-done | bytes 4194320 | tf_op jit(solution)/shard_map/all_gather | solution.py:47
  173.2 6.1 %fusion.1 = f32[256,256]{1,0:T(8,128)S(1)} fusion(bf16[8192,256]{1,0:T(8,128)(2,1)} %all-gather.4.cloned.1.call-done, bf16[256,8192]{1,0:T(8,128)(2,1)} %param.10, bf16[256,8192]{1,0:T(8,128)(2,1)} %param.9, f32[256]{0:T(256)S(1)} %copy-done.3), kind=kOutput, calls=%fused_computation.4 | convolution fusion | flops 1084227584 | bytes 12846080 | tf_op jit(solution)/shard_map/dot_general | solution.py:45
  179.4 0.3 fusion.46
  179.7 6.7 %fusion = f32[8192,256]{0,1:T(8,128)} fusion(bf16[256,256]{1,0:T(8,128)(2,1)S(1)} %fusion.46, bf16[256,8192]{1,0:T(8,128)(2,1)} %param.9), kind=kOutput, calls=%fused_computation.2 | convolution fusion | flops 1075838976 | bytes 12713984 | tf_op jit(solution)/shard_map/dot_general | solution.py:60
  186.4 0.0 reduce-scatter.2.cloned.1.call-update
  186.4 0.0 all-reduce.2.cloned.1.call-start
  186.5 70.0 %reduce-scatter.2.cloned.1.call-done = f32[1024,256]{0,1:T(8,128)} async-done(((f32[8192,256]{0,1:T(8,128)}), f32[1024,256]{0,1:T(8,128)}) %reduce-scatter.2.cloned.1.call-update) | async-done | bytes 1048592 | tf_op jit(solution)/shard_map/reduce_scatter | solution.py:59
  256.5 0.0 all-reduce.2.cloned.1.call-update
  256.5 0.0 all-gather.8.cloned.1.call-start
  256.5 54.1 %all-reduce.2.cloned.1.call-done = f32[1024,256]{0,1:T(8,128)} async-done(((f32[1024,256]{0,1:T(8,128)}), f32[1024,256]{0,1:T(8,128)}) %all-reduce.2.cloned.1.call-update) | async-done | bytes 1048592 | tf_op jit(solution)/shard_map/psum | solution.py:68
  310.6 0.0 all-gather.8.cloned.1.call-update
  310.6 0.7 multiply_bitcast_fusion
  311.3 0.1 fusion.70
  311.4 0.7 compare_bitcast_fusion
  312.2 0.1 fusion.74
  312.3 53.6 %all-gather.8.cloned.1.call-done = f32[8192,256]{0,1:T(8,128)} async-done(((f32[1024,256]{0,1:T(8,128)}), f32[8192,256]{0,1:T(8,128)}) %all-gather.8.cloned.1.call-update) | async-done | bytes 8388624 | tf_op jit(solution)/shard_map/all_gather | solution.py:73
  365.9 9.0 %copy.10 = f32[8192,256]{1,0:T(8,128)} copy(f32[8192,256]{0,1:T(8,128)} %all-gather.8.cloned.1.call-done) | data formatting | bytes 16777216 | tf_op jit(solution)/shard_map/all_gather | solution.py:73
  374.9 10.0 %gather_fusion = f32[2048,256]{1,0:T(8,128)S(1)} fusion(f32[8192,256]{1,0:T(8,128)} %copy.10, s32[2048]{0:T(1024)S(1)} %broadcast_clamp_fusion), kind=kCustom, calls=%fused_computation | custom fusion | bytes 4202496 | tf_op jit(solution)/shard_map/jit(_take)/gather | solution.py:76
  384.9 0.0 copy-start.2
  384.9 6.5 %multiply_add_fusion = f32[8,256,256]{2,1,0:T(8,128)S(1)} fusion(f32[8,256,256]{2,1,0:T(8,128)} %param.17, f32[8,256,256]{2,1,0:T(8,128)S(1)} %bitcast.43, pred[8]{0:T(512)(128)(4,1)S(1)} %compare_bitcast_fusion, pred[8,256]{1,0:T(8,128)(4,1)S(1)} %get-tuple-element.8, pred[8,256]{1,0:T(8,128)(4,1)S(1)} %get-tuple-element.7), kind=kOutput, calls=%fused_computation.46 | convolution fusion | flops 1613758464 | bytes 6295560 | tf_op jit(solution)/shard_map/kij,kjl->kil/dot_general | solution.py:13
  391.4 4.4 multiply_add_fusion.1
  395.8 0.6 multiply_reduce_fusion
  396.5 6.1 %fusion.8 = f32[16,256,256]{2,1,0:T(8,128)S(1)} fusion(f32[256,256]{1,0:T(8,128)S(1)} %get-tuple-element.9, f32[8,256,256]{2,1,0:T(8,128)S(1)} %multiply_add_fusion, f32[8,256,256]{2,1,0:T(8,128)S(1)} %multiply_add_fusion.1, f32[16]{0:T(128)S(1)} %get-tuple-element.5, f32[256,256]{1,0:T(8,128)S(1)} %get-tuple-element.10), kind=kOutput, calls=%fused_computation.17 | convolution fusion | flops 3226468352 | bytes 8912960 | tf_op jit(solution)/shard_map/kij,kjl->kil/dot_general | solution.py:13
  402.6 5.1 %fusion.96 = f32[16,256,256]{2,1,0:T(8,128)S(1)} fusion(f32[16,256,256]{2,1,0:T(8,128)S(1)} %fusion.8), kind=kOutput, calls=%fused_computation.115 | convolution fusion | flops 3221225472 | bytes 8388608 | tf_op jit(solution)/shard_map/kij,kjl->kil/dot_general | solution.py:13
  407.7 5.4 %fusion.92 = f32[16,256,256]{2,1,0:T(8,128)S(1)} fusion(f32[16,256,256]{2,1,0:T(8,128)S(1)} %fusion.96, f32[8,256,256]{2,1,0:T(8,128)S(1)} %multiply_add_fusion, f32[8,256,256]{2,1,0:T(8,128)S(1)} %multiply_add_fusion.1, f32[16]{0:T(128)S(1)} %get-tuple-element.5, f32[256,256]{1,0:T(8,128)S(1)} %get-tuple-element.10), kind=kOutput, calls=%fused_computation.113 | convolution fusion | flops 3224371200 | bytes 12845120 | tf_op jit(solution)/shard_map/kij,kjl->kil/dot_general | solution.py:13
  413.1 5.7 %fusion.9 = f32[16,256,256]{2,1,0:T(8,128)S(1)} fusion(f32[16,256,256]{2,1,0:T(8,128)S(1)} %fusion.92, f32[256,256]{1,0:T(8,128)S(1)} %get-tuple-element.9), kind=kOutput, calls=%fused_computation.18 | convolution fusion | flops 3223322624 | bytes 8650752 | tf_op jit(solution)/shard_map/kij,kjl->kil/dot_general | solution.py:13
  418.8 6.0 %fusion.5 = f32[16,256,256]{2,1,0:T(8,128)S(1)} fusion(f32[256,256]{1,0:T(8,128)S(1)} %get-tuple-element.9, f32[16]{0:T(128)S(1)} %get-tuple-element.6, f32[256,256]{1,0:T(8,128)S(1)} %fusion.65, f32[8,256,256]{2,1,0:T(8,128)S(1)} %multiply_add_fusion, f32[8,256,256]{2,1,0:T(8,128)S(1)} %multiply_add_fusion.1, f32[16]{0:T(128)S(1)} %get-tuple-element.5, ...), kind=kOutput, calls=%fused_computation.13 | convolution fusion | flops 3227516928 | bytes 9175168 | tf_op jit(solution)/shard_map/kij,kjl->kil/dot_general | solution.py:13
  424.8 5.3 %fusion.10 = f32[16,256,256]{2,1,0:T(8,128)S(1)} fusion(f32[16,256,256]{2,1,0:T(8,128)S(1)} %fusion.5, f32[16,256,256]{2,1,0:T(8,128)S(1)} %fusion.92, f32[256,256]{1,0:T(8,128)S(1)} %get-tuple-element.9), kind=kOutput, calls=%fused_computation.19 | convolution fusion | flops 3223322624 | bytes 12845056 | tf_op jit(solution)/shard_map/kij,kjl->kil/dot_general | solution.py:13
  430.1 5.1 %fusion.97 = f32[16,256,256]{2,1,0:T(8,128)S(1)} fusion(f32[16,256,256]{2,1,0:T(8,128)S(1)} %fusion.9), kind=kOutput, calls=%fused_computation.116 | convolution fusion | flops 3221225472 | bytes 8388608 | tf_op jit(solution)/shard_map/kij,kjl->kil/dot_general | solution.py:13
  435.2 5.2 %fusion.98 = f32[16,256,256]{2,1,0:T(8,128)S(1)} fusion(f32[16,256,256]{2,1,0:T(8,128)S(1)} %fusion.97, f32[16,256,256]{2,1,0:T(8,128)S(1)} %fusion.92), kind=kOutput, calls=%fused_computation.117 | convolution fusion | flops 3221225472 | bytes 12582912 | tf_op jit(solution)/shard_map/kij,kjl->kil/dot_general | solution.py:13
  440.4 5.6 %fusion.11 = f32[16,256,256]{2,1,0:T(8,128)S(1)} fusion(f32[16,256,256]{2,1,0:T(8,128)S(1)} %fusion.98, f32[256,256]{1,0:T(8,128)S(1)} %get-tuple-element.9), kind=kOutput, calls=%fused_computation.20 | convolution fusion | flops 3223322624 | bytes 8650752 | tf_op jit(solution)/shard_map/kij,kjl->kil/dot_general | solution.py:13
  446.0 5.4 %fusion.12 = f32[16,256,256]{2,1,0:T(8,128)S(1)} fusion(f32[16,256,256]{2,1,0:T(8,128)S(1)} %fusion.10, f32[16,256,256]{2,1,0:T(8,128)S(1)} %fusion.98, f32[256,256]{1,0:T(8,128)S(1)} %get-tuple-element.9), kind=kOutput, calls=%fused_computation.21 | convolution fusion | flops 3223322624 | bytes 12845056 | tf_op jit(solution)/shard_map/kij,kjl->kil/dot_general | solution.py:13
  451.4 5.0 fusion.99
  456.4 5.0 %fusion.100 = f32[16,256,256]{2,1,0:T(8,128)S(1)} fusion(f32[16,256,256]{2,1,0:T(8,128)S(1)} %fusion.99, f32[16,256,256]{2,1,0:T(8,128)S(1)} %fusion.98), kind=kOutput, calls=%fused_computation.119 | convolution fusion | flops 3221225472 | bytes 12582912 | tf_op jit(solution)/shard_map/kij,kjl->kil/dot_general | solution.py:13
  461.4 6.0 %fusion.13 = f32[16,256,256]{2,1,0:T(8,128)S(1)} fusion(f32[16,256,256]{2,1,0:T(8,128)S(1)} %fusion.100, f32[256,256]{1,0:T(8,128)S(1)} %get-tuple-element.9), kind=kOutput, calls=%fused_computation.22 | convolution fusion | flops 3223322624 | bytes 8650752 | tf_op jit(solution)/shard_map/kij,kjl->kil/dot_general | solution.py:13
  467.4 5.1 %fusion.14 = f32[16,256,256]{2,1,0:T(8,128)S(1)} fusion(f32[16,256,256]{2,1,0:T(8,128)S(1)} %fusion.12, f32[16,256,256]{2,1,0:T(8,128)S(1)} %fusion.100, f32[256,256]{1,0:T(8,128)S(1)} %get-tuple-element.9), kind=kOutput, calls=%fused_computation.23 | convolution fusion | flops 3223322624 | bytes 12845056 | tf_op jit(solution)/shard_map/kij,kjl->kil/dot_general | solution.py:13
  472.5 5.1 %fusion.101 = f32[16,256,256]{2,1,0:T(8,128)S(1)} fusion(f32[16,256,256]{2,1,0:T(8,128)S(1)} %fusion.13), kind=kOutput, calls=%fused_computation.120 | convolution fusion | flops 3221225472 | bytes 8388608 | tf_op jit(solution)/shard_map/kij,kjl->kil/dot_general | solution.py:13
  477.6 5.0 %fusion.102 = f32[16,256,256]{2,1,0:T(8,128)S(1)} fusion(f32[16,256,256]{2,1,0:T(8,128)S(1)} %fusion.101, f32[16,256,256]{2,1,0:T(8,128)S(1)} %fusion.100), kind=kOutput, calls=%fused_computation.121 | convolution fusion | flops 3221225472 | bytes 12582912 | tf_op jit(solution)/shard_map/kij,kjl->kil/dot_general | solution.py:13
  482.7 5.1 %fusion.2 = f32[16,256,256]{2,1,0:T(8,128)S(1)} fusion(f32[16,256,256]{2,1,0:T(8,128)S(1)} %fusion.14, f32[16,256,256]{2,1,0:T(8,128)S(1)} %fusion.102, f32[256,256]{1,0:T(8,128)S(1)} %get-tuple-element.9), kind=kOutput, calls=%fused_computation.6 | convolution fusion | flops 3223322624 | bytes 12845056 | tf_op jit(solution)/shard_map/kij,kjl->kil/dot_general | solution.py:13
  487.8 0.0 copy-start.1
  487.8 2.8 fusion.41
  490.6 3.5 fusion.38
  (13 shorter events, 0.1 us)
Async XLA Ops:
  6.5 172.8 %copy-start = (bf16[256,256]{1,0:T(8,128)(2,1)S(1)}, bf16[256,256]{1,0:T(8,128)(2,1)}, u32[]{:S(2)}) copy-start(bf16[256,256]{1,0:T(8,128)(2,1)} %param.14) | copy-start | bytes 393220
  6.5 85.9 %all-gather.6.cloned.1.call-start = ((), (), s32[]{:S(2)}) async-start(), calls=%async_computation.2 | async-start | bytes 5242880 | tf_op jit(solution)/shard_map/all_gather | solution.py:42
  7.3 166.0 %all-gather.4.cloned.1.call-start = ((), (), s32[]{:S(2)}) async-start(), calls=%async_computation.1 | async-start | bytes 5242880 | tf_op jit(solution)/shard_map/all_gather | solution.py:47
  8.0 165.2 %copy-start.3 = (f32[256]{0:T(256)S(1)}, f32[256]{0:T(256)}, u32[]{:S(2)}) copy-start(f32[256]{0:T(256)} %param.11) | copy-start | bytes 3076
  8.0 248.4 %reduce-scatter.2.cloned.1.call-start = ((), (), s32[]{:S(2)}) async-start(), calls=%async_computation.3 | async-start | bytes 9437184 | tf_op jit(solution)/shard_map/reduce_scatter | solution.py:59
  186.4 124.1 %all-reduce.2.cloned.1.call-start = ((), (), s32[]{:S(2)}) async-start(), calls=%async_computation.4 | async-start | bytes 2097152 | tf_op jit(solution)/shard_map/psum | solution.py:68
  256.5 109.4 %all-gather.8.cloned.1.call-start = ((), (), s32[]{:S(2)}) async-start(), calls=%async_computation.5 | async-start | bytes 9437184 | tf_op jit(solution)/shard_map/all_gather | solution.py:73
  384.9 6.5 %copy-start.2 = (f32[8,256,256]{2,1,0:T(8,128)S(1)}, f32[8,256,256]{2,1,0:T(8,128)}, u32[]{:S(2)}) copy-start(f32[8,256,256]{2,1,0:T(8,128)} %param.16) | copy-start | bytes 6291460
  487.8 6.3 %copy-start.1 = (bf16[256,256]{1,0:T(8,128)(2,1)S(1)}, bf16[256,256]{1,0:T(8,128)(2,1)}, u32[]{:S(2)}) copy-start(bf16[256,256]{1,0:T(8,128)(2,1)} %param.14) | copy-start | bytes 393220
Sparse Core Ops, SparseCore 0:
  8.9 83.4 all-gather.5
  94.0 79.2 all-gather.3
  186.6 69.8 reduce-scatter.1
  258.7 51.8 all-reduce.1
  312.3 53.5 all-gather.7
where the time goes:
time: 507 us; the launch traced here: 501 us
  waiting for transfers between devices  340 us (67%)
  matrix products  126 us (25%)
  local copies, waits for them, and re-layouts  19 us (4%)
  between operations  13.6 us (3%)
    dot_general x21, matrix products, batched(): jnp.einsum('kij,kjl->kil', left, right, precision=lax.Precision.HIGHEST)  108 us
    all_gather x1, waiting for transfers between devices, shards(): lax.all_gather(down_weight, 'rep', axis=0, tiled=True)  84.3 us
    all_gather x1, waiting for transfers between devices, shards(): lax.all_gather(up_weight, 'rep', axis=0, tiled=True)  76.1 us
    reduce_scatter x1, waiting for transfers between devices, shards(): lax.psum_scatter(lax.dot_general(columns, signal, (((0,), (0,)), ((), ())...  70 us
    psum x1, waiting for transfers between devices, shards(): shard = lax.psum(shard, 'rep')  54.1 us
    all_gather x1, waiting for transfers between devices, shards(): shard_rows = lax.all_gather(shard, 'own', axis=0, tiled=True)  53.6 us
  transfers between devices with their start and end apart: 5, of which 5 were waited for; matrix products, arithmetic and copies ran while one was open for 1% of the time, Pallas kernels for 0%

commit v1 on v0

--- a/solution.py
+++ b/solution.py
@@ -65,7 +65,9 @@
         scatter_dimension=0,
         tiled=True,
     )
-    shard = lax.psum(shard, "rep")
+    shard = shard
+    for hop in (1, 2):
+        shard = shard + lax.ppermute(shard, "rep", [(dev, dev ^ hop) for dev in range(4)])
     my_blocks = lax.dynamic_index_in_dim(owner_table, lax.axis_index("own"), 0, keepdims=False)
     wanted = (
         jnp.maximum(my_blocks, 0)[:, None] * R + jnp.arange(R, dtype=jnp.int32)[None, :]

time: 507 us -> 527 us (1.039)
  waiting for transfers between devices: 340 us -> 353 us
    ppermute x0 -> x2, waiting for transfers between devices: none -> 68.3 us  [shards(): lax.ppermute(shard, 'rep', [(dev, dev ^ hop) for dev in range(4)])]
    psum x1 -> x0, waiting for transfers between devices: 54.1 us -> none  [shards(): shard = lax.psum(shard, 'rep')]
  transfers between devices with their start and end apart: 5 -> 6, of which waited for: 5 -> 6; matrix products, arithmetic and copies ran while one was open for 1% -> 1% of each run, Pallas kernels for 0% -> 0%
where the time goes in v1:
time: 527 us; the launch traced here: 521 us
  waiting for transfers between devices  353 us (67%)
  matrix products  126 us (24%)
  local copies, waits for them, and re-layouts  19 us (4%)
  between operations  13.6 us (3%)
    dot_general x21, matrix products, batched(): jnp.einsum('kij,kjl->kil', left, right, precision=lax.Precision.HIGHEST)  108 us
    all_gather x1, waiting for transfers between devices, shards(): lax.all_gather(down_weight, 'rep', axis=0, tiled=True)  84.3 us
    all_gather x1, waiting for transfers between devices, shards(): lax.all_gather(up_weight, 'rep', axis=0, tiled=True)  76.1 us
    reduce_scatter x1, waiting for transfers between devices, shards(): lax.psum_scatter(lax.dot_general(columns, signal, (((0,), (0,)), ((), ())...  70 us
    ppermute x2, waiting for transfers between devices, shards(): lax.ppermute(shard, 'rep', [(dev, dev ^ hop) for dev in range(4)])  68.3 us
    all_gather x1, waiting for transfers between devices, shards(): shard_rows = lax.all_gather(shard, 'own', axis=0, tiled=True)  52.7 us
  transfers between devices with their start and end apart: 6, of which 6 were waited for; matrix products, arithmetic and copies ran while one was open for 1% of the time, Pallas kernels for 0%

profile of v1, /device:TPU:0, one launch (start us, length us, event | category | flops | bytes accessed | tf_op | source)
XLA Modules:
  0.0 520.5 jit_solution(1265078218059268078)
XLA Ops:
  6.5 0.7 all-gather.6.cloned.1.call-update
  7.3 0.0 all-gather.4.cloned.1.call-start
  7.3 0.7 all-gather.4.cloned.1.call-update
  8.0 0.0 reduce-scatter.2.cloned.1.call-start
  8.1 84.3 %all-gather.6.cloned.1.call-done = bf16[8192,256]{1,0:T(8,128)(2,1)} async-done(((bf16[2048,256]{1,0:T(8,128)(2,1)}), bf16[8192,256]{1,0:T(8,128)(2,1)}) %all-gather.6.cloned.1.call-update) | async-done | bytes 4194320 | tf_op jit(solution)/shard_map/all_gather | solution.py:42
  92.4 4.7 fusion.47
  97.1 76.1 %all-gather.4.cloned.1.call-done = bf16[8192,256]{1,0:T(8,128)(2,1)} async-done(((bf16[2048,256]{1,0:T(8,128)(2,1)}), bf16[8192,256]{1,0:T(8,128)(2,1)}) %all-gather.4.cloned.1.call-update) | async-done | bytes 4194320 | tf_op jit(solution)/shard_map/all_gather | solution.py:47
  173.2 6.1 %fusion.1 = f32[256,256]{1,0:T(8,128)S(1)} fusion(bf16[8192,256]{1,0:T(8,128)(2,1)} %all-gather.4.cloned.1.call-done, bf16[256,8192]{1,0:T(8,128)(2,1)} %param.10, bf16[256,8192]{1,0:T(8,128)(2,1)} %param.9, f32[256]{0:T(256)S(1)} %copy-done.3), kind=kOutput, calls=%fused_computation.4 | convolution fusion | flops 1084227584 | bytes 12846080 | tf_op jit(solution)/shard_map/dot_general | solution.py:45
  179.4 0.3 fusion.46
  179.7 6.7 %fusion = f32[8192,256]{0,1:T(8,128)} fusion(bf16[256,256]{1,0:T(8,128)(2,1)S(1)} %fusion.46, bf16[256,8192]{1,0:T(8,128)(2,1)} %param.9), kind=kOutput, calls=%fused_computation.2 | convolution fusion | flops 1075838976 | bytes 12713984 | tf_op jit(solution)/shard_map/dot_general | solution.py:60
  186.4 0.0 reduce-scatter.2.cloned.1.call-update
  186.4 0.0 all-gather.8.cloned.1.call-start
  186.5 70.0 %reduce-scatter.2.cloned.1.call-done = f32[1024,256]{0,1:T(8,128)} async-done(((f32[8192,256]{0,1:T(8,128)}), f32[1024,256]{0,1:T(8,128)}) %reduce-scatter.2.cloned.1.call-update) | async-done | bytes 1048592 | tf_op jit(solution)/shard_map/reduce_scatter | solution.py:59
  256.4 1.5 collective-permute-start
  257.9 23.4 %collective-permute-done = f32[1024,256]{0,1:T(8,128)S(1)} collective-permute-done((f32[1024,256]{0,1:T(8,128)}, f32[1024,256]{0,1:T(8,128)S(1)}, u32[]{:S(2)}, u32[]{:S(2)}) %collective-permute-start) | collective-permute-done | bytes 1048608 | tf_op jit(solution)/shard_map/ppermute | solution.py:70
  281.4 1.4 add.78
  282.7 2.5 collective-permute-start.1
  285.2 44.8 %collective-permute-done.1 = f32[1024,256]{0,1:T(8,128)S(1)} collective-permute-done((f32[1024,256]{0,1:T(8,128)S(1)}, f32[1024,256]{0,1:T(8,128)S(1)}, u32[]{:S(2)}, u32[]{:S(2)}) %collective-permute-start.1) | collective-permute-done | bytes 1048608 | tf_op jit(solution)/shard_map/ppermute | solution.py:70
  330.0 1.1 add.79
  331.2 0.7 multiply_bitcast_fusion
  331.9 0.1 fusion.70
  332.0 0.7 compare_bitcast_fusion
  332.7 0.1 fusion.74
  332.8 52.7 %all-gather.8.cloned.1.call-done = f32[8192,256]{0,1:T(8,128)} async-done(((f32[1024,256]{0,1:T(8,128)}), f32[8192,256]{0,1:T(8,128)}) %all-gather.8.cloned.1.call-update) | async-done | bytes 8388624 | tf_op jit(solution)/shard_map/all_gather | solution.py:75
  385.6 9.0 %copy.10 = f32[8192,256]{1,0:T(8,128)} copy(f32[8192,256]{0,1:T(8,128)} %all-gather.8.cloned.1.call-done) | data formatting | bytes 16777216 | tf_op jit(solution)/shard_map/all_gather | solution.py:75
  394.6 10.0 %gather_fusion = f32[2048,256]{1,0:T(8,128)S(1)} fusion(f32[8192,256]{1,0:T(8,128)} %copy.10, s32[2048]{0:T(1024)S(1)} %broadcast_clamp_fusion), kind=kCustom, calls=%fused_computation | custom fusion | bytes 4202496 | tf_op jit(solution)/shard_map/jit(_take)/gather | solution.py:78
  404.6 6.5 %multiply_add_fusion = f32[8,256,256]{2,1,0:T(8,128)S(1)} fusion(f32[8,256,256]{2,1,0:T(8,128)} %param.17, f32[8,256,256]{2,1,0:T(8,128)S(1)} %bitcast.43, pred[8]{0:T(512)(128)(4,1)S(1)} %compare_bitcast_fusion, pred[8,256]{1,0:T(8,128)(4,1)S(1)} %get-tuple-element.8, pred[8,256]{1,0:T(8,128)(4,1)S(1)} %get-tuple-element.7), kind=kOutput, calls=%fused_computation.46 | convolution fusion | flops 1613758464 | bytes 6295560 | tf_op jit(solution)/shard_map/kij,kjl->kil/dot_general | solution.py:13
  411.1 4.4 multiply_add_fusion.1
  415.5 0.6 multiply_reduce_fusion
  416.2 6.1 %fusion.8 = f32[16,256,256]{2,1,0:T(8,128)S(1)} fusion(f32[256,256]{1,0:T(8,128)S(1)} %get-tuple-element.9, f32[8,256,256]{2,1,0:T(8,128)S(1)} %multiply_add_fusion, f32[8,256,256]{2,1,0:T(8,128)S(1)} %multiply_add_fusion.1, f32[16]{0:T(128)S(1)} %get-tuple-element.5, f32[256,256]{1,0:T(8,128)S(1)} %get-tuple-element.10), kind=kOutput, calls=%fused_computation.17 | convolution fusion | flops 3226468352 | bytes 8912960 | tf_op jit(solution)/shard_map/kij,kjl->kil/dot_general | solution.py:13
  422.3 5.1 fusion.96
  427.4 5.4 %fusion.92 = f32[16,256,256]{2,1,0:T(8,128)S(1)} fusion(f32[16,256,256]{2,1,0:T(8,128)S(1)} %fusion.96, f32[8,256,256]{2,1,0:T(8,128)S(1)} %multiply_add_fusion, f32[8,256,256]{2,1,0:T(8,128)S(1)} %multiply_add_fusion.1, f32[16]{0:T(128)S(1)} %get-tuple-element.5, f32[256,256]{1,0:T(8,128)S(1)} %get-tuple-element.10), kind=kOutput, calls=%fused_computation.113 | convolution fusion | flops 3224371200 | bytes 12845120 | tf_op jit(solution)/shard_map/kij,kjl->kil/dot_general | solution.py:13
  432.8 5.7 %fusion.9 = f32[16,256,256]{2,1,0:T(8,128)S(1)} fusion(f32[16,256,256]{2,1,0:T(8,128)S(1)} %fusion.92, f32[256,256]{1,0:T(8,128)S(1)} %get-tuple-element.9), kind=kOutput, calls=%fused_computation.18 | convolution fusion | flops 3223322624 | bytes 8650752 | tf_op jit(solution)/shard_map/kij,kjl->kil/dot_general | solution.py:13
  438.5 6.0 %fusion.5 = f32[16,256,256]{2,1,0:T(8,128)S(1)} fusion(f32[256,256]{1,0:T(8,128)S(1)} %get-tuple-element.9, f32[16]{0:T(128)S(1)} %get-tuple-element.6, f32[256,256]{1,0:T(8,128)S(1)} %fusion.65, f32[8,256,256]{2,1,0:T(8,128)S(1)} %multiply_add_fusion, f32[8,256,256]{2,1,0:T(8,128)S(1)} %multiply_add_fusion.1, f32[16]{0:T(128)S(1)} %get-tuple-element.5, ...), kind=kOutput, calls=%fused_computation.13 | convolution fusion | flops 3227516928 | bytes 9175168 | tf_op jit(solution)/shard_map/kij,kjl->kil/dot_general | solution.py:13
  444.5 5.3 %fusion.10 = f32[16,256,256]{2,1,0:T(8,128)S(1)} fusion(f32[16,256,256]{2,1,0:T(8,128)S(1)} %fusion.5, f32[16,256,256]{2,1,0:T(8,128)S(1)} %fusion.92, f32[256,256]{1,0:T(8,128)S(1)} %get-tuple-element.9), kind=kOutput, calls=%fused_computation.19 | convolution fusion | flops 3223322624 | bytes 12845056 | tf_op jit(solution)/shard_map/kij,kjl->kil/dot_general | solution.py:13
  449.8 5.1 fusion.97
  454.9 5.2 %fusion.98 = f32[16,256,256]{2,1,0:T(8,128)S(1)} fusion(f32[16,256,256]{2,1,0:T(8,128)S(1)} %fusion.97, f32[16,256,256]{2,1,0:T(8,128)S(1)} %fusion.92), kind=kOutput, calls=%fused_computation.117 | convolution fusion | flops 3221225472 | bytes 12582912 | tf_op jit(solution)/shard_map/kij,kjl->kil/dot_general | solution.py:13
  460.2 5.6 %fusion.11 = f32[16,256,256]{2,1,0:T(8,128)S(1)} fusion(f32[16,256,256]{2,1,0:T(8,128)S(1)} %fusion.98, f32[256,256]{1,0:T(8,128)S(1)} %get-tuple-element.9), kind=kOutput, calls=%fused_computation.20 | convolution fusion | flops 3223322624 | bytes 8650752 | tf_op jit(solution)/shard_map/kij,kjl->kil/dot_general | solution.py:13
  465.7 5.4 %fusion.12 = f32[16,256,256]{2,1,0:T(8,128)S(1)} fusion(f32[16,256,256]{2,1,0:T(8,128)S(1)} %fusion.10, f32[16,256,256]{2,1,0:T(8,128)S(1)} %fusion.98, f32[256,256]{1,0:T(8,128)S(1)} %get-tuple-element.9), kind=kOutput, calls=%fused_computation.21 | convolution fusion | flops 3223322624 | bytes 12845056 | tf_op jit(solution)/shard_map/kij,kjl->kil/dot_general | solution.py:13
  471.1 5.0 fusion.99
  476.1 5.0 fusion.100
  481.1 6.0 %fusion.13 = f32[16,256,256]{2,1,0:T(8,128)S(1)} fusion(f32[16,256,256]{2,1,0:T(8,128)S(1)} %fusion.100, f32[256,256]{1,0:T(8,128)S(1)} %get-tuple-element.9), kind=kOutput, calls=%fused_computation.22 | convolution fusion | flops 3223322624 | bytes 8650752 | tf_op jit(solution)/shard_map/kij,kjl->kil/dot_general | solution.py:13
  487.1 5.1 fusion.14
  492.2 5.1 fusion.101
  497.3 5.0 fusion.102
  502.4 5.1 fusion.2
  507.5 2.8 fusion.41
  510.3 3.5 fusion.38
  (16 shorter events, 0.1 us)
Async XLA Ops:
  6.5 172.8 %copy-start = (bf16[256,256]{1,0:T(8,128)(2,1)S(1)}, bf16[256,256]{1,0:T(8,128)(2,1)}, u32[]{:S(2)}) copy-start(bf16[256,256]{1,0:T(8,128)(2,1)} %param.14) | copy-start | bytes 393220
  6.5 85.9 %all-gather.6.cloned.1.call-start = ((), (), s32[]{:S(2)}) async-start(), calls=%async_computation.2 | async-start | bytes 5242880 | tf_op jit(solution)/shard_map/all_gather | solution.py:42
  7.3 166.0 %all-gather.4.cloned.1.call-start = ((), (), s32[]{:S(2)}) async-start(), calls=%async_computation.1 | async-start | bytes 5242880 | tf_op jit(solution)/shard_map/all_gather | solution.py:47
  8.0 165.2 %copy-start.3 = (f32[256]{0:T(256)S(1)}, f32[256]{0:T(256)}, u32[]{:S(2)}) copy-start(f32[256]{0:T(256)} %param.11) | copy-start | bytes 3076
  8.0 248.4 %reduce-scatter.2.cloned.1.call-start = ((), (), s32[]{:S(2)}) async-start(), calls=%async_computation.3 | async-start | bytes 9437184 | tf_op jit(solution)/shard_map/reduce_scatter | solution.py:59
  186.4 199.2 %all-gather.8.cloned.1.call-start = ((), (), s32[]{:S(2)}) async-start(), calls=%async_computation.4 | async-start | bytes 9437184 | tf_op jit(solution)/shard_map/all_gather | solution.py:75
  256.4 24.9 %collective-permute-start = (f32[1024,256]{0,1:T(8,128)}, f32[1024,256]{0,1:T(8,128)S(1)}, u32[]{:S(2)}, u32[]{:S(2)}) collective-permute-start(f32[1024,256]{0,1:T(8,128)} %reduce-scatter.2.cloned.1.call-done), channel_id=1, source_target_pairs={{0,8},{8,0},{16,24},{24,16},{1,9},{9,1},{17,25},{25,17},{2,10},{10... | collective-permute-start | bytes 3145736 | tf_op jit(solution)/shard_map/ppermute | solution.py:70
  282.7 47.3 %collective-permute-start.1 = (f32[1024,256]{0,1:T(8,128)S(1)}, f32[1024,256]{0,1:T(8,128)S(1)}, u32[]{:S(2)}, u32[]{:S(2)}) collective-permute-start(f32[1024,256]{0,1:T(8,128)S(1)} %add.78), channel_id=1, source_target_pairs={{0,16},{8,24},{16,0},{24,8},{1,17},{9,25},{17,1},{25,9},{2,18},{10... | collective-permute-start | bytes 3145736 | tf_op jit(solution)/shard_map/ppermute | solution.py:70
  404.6 6.5 %copy-start.2 = (f32[8,256,256]{2,1,0:T(8,128)S(1)}, f32[8,256,256]{2,1,0:T(8,128)}, u32[]{:S(2)}) copy-start(f32[8,256,256]{2,1,0:T(8,128)} %param.16) | copy-start | bytes 6291460
  507.5 6.3 %copy-start.1 = (bf16[256,256]{1,0:T(8,128)(2,1)S(1)}, bf16[256,256]{1,0:T(8,128)(2,1)}, u32[]{:S(2)}) copy-start(bf16[256,256]{1,0:T(8,128)(2,1)} %param.14) | copy-start | bytes 393220
Sparse Core Ops, SparseCore 0:
  8.9 83.4 all-gather.5
  94.0 79.2 all-gather.3
  186.5 69.8 reduce-scatter.1
  331.3 54.2 all-gather.7
